TPU v7x, 32 devices: a whole 2x2x4 slice. The times are simulated.
32 devices in a mesh: loader: 8 (over z, x), split: 4 (over y, core).
Axes of the slice: x: 2, y: 2, z: 4, core: 2. Of those that a mesh axis runs over, the one named last changes fastest.
Arguments:
- embeddings: bfloat16 [16384, 768], P(('loader', 'split')), may hold values from -6 to 6
- cluster_ids: int32 [16384, 1], P(('loader', 'split')), may hold values from 0 to 255; in each aligned block of 512 rows (0 to 511, 512 to 1023, ...) at most 4 rows name the same one
- ranks: int32 [16384], P(('loader', 'split')), may hold values from 0 to 16383, each once
Outputs:
- nearest: float32 [16384], P(('loader', 'split'))
Inputs may be any that keep to these rules, and one draw needn't show every extreme that they name: `cluster_ids`: among the 512 rows of one device no cluster appears more than 4 times. All ranks differ.
All inputs are finite; a program needn't handle non-finite values.
Results may differ from a plain program's by a relative error of at most 0.0014.
Values may be sent and summed in bfloat16 or wider, within the bound.
A program may use at most 64 MiB of HBM per device.

v0:
```python
import functools

import jax
import jax.numpy as jnp
from jax import lax
from jax.experimental import pallas as pl
from jax.experimental.pallas import tpu as pltpu
from jax.sharding import PartitionSpec as P

CLUSTERS = 256
CAP = 4
LANES = 128
TILE = 16

epsilon = 1e-06
EXACT = lax.Precision.HIGHEST
NN = (((1,), (0,)), ((), ()))
NT = (((1,), (1,)), ((), ()))
TN = (((0,), (0,)), ((), ()))
QUARTERS = (2, 1, 3, 0)


def dot(a, b, dims, precision=None):
    return lax.dot_general(a, b, dims, precision=precision, preferred_element_type=jnp.float32)


def iota(shape, axis):
    return lax.broadcasted_iota(jnp.int32, shape, axis)


def column(row):
    return jnp.transpose(jnp.broadcast_to(row, (LANES, row.shape[1])))[:, :1]


def kernel(n, splits, chunks, big, emb_hbm, cid_hbm, rank_hbm, out_ref, over_ref, *scratch):
    pieces = len(chunks)
    rows_out, rows_in = scratch[:pieces], scratch[pieces : 2 * pieces]
    (
        keys_out, keys_in, best_out, best_in,
        rows_out_sem, rows_in_sem, keys_out_sem, keys_in_sem, best_out_sem, best_in_sem, own_sem,
        emb_ref, cid_ref, rank_ref, load_sem,
    ) = scratch[2 * pieces :]
    me = lax.axis_index("loader") * splits + lax.axis_index("split")
    count, width = emb_hbm.shape
    quarter = n // 4
    mine, inner = me // quarter, me % quarter
    sign = 1 - 2 * (mine // 2)
    starts = [sum(chunks[:i]) for i in range(pieces)]

    def where_is(index):
        return {"loader": index // splits, "split": index % splits}

    def quarter_of(turn):
        return (mine + sign * QUARTERS[turn] + 4) % 4

    def each(act, turns=range(4)):
        for turn in turns:
            base = quarter_of(turn) * quarter
            first = 1 if QUARTERS[turn] == 0 else 0

            def step(i, carry):
                act(base + (inner + i) % quarter)
                return carry

            lax.fori_loop(first, quarter, step, 0)

    def remote(source, target, send, receive, peer):
        return pltpu.make_async_remote_copy(
            src_ref=source, dst_ref=target, send_sem=send, recv_sem=receive,
            device_id=where_is(peer), device_id_type=pl.DeviceIdType.MESH,
        )

    barrier = pltpu.get_barrier_semaphore()
    each(
        lambda peer: pl.semaphore_signal(
            barrier, inc=1, device_id=where_is(peer), device_id_type=pl.DeviceIdType.MESH
        )
    )

    loads = [
        pltpu.make_async_copy(source, target, load_sem.at[i])
        for i, (source, target) in enumerate(
            ((cid_hbm, cid_ref), (rank_hbm, rank_ref), (emb_hbm, emb_ref))
        )
    ]
    for load in loads:
        load.start()
    loads[0].wait()

    owner = cid_ref[...] % n
    before = (column(owner) == owner) & (iota((count, count), 0) < iota((count, count), 1))
    place = jnp.sum(before.astype(jnp.int32), axis=0, keepdims=True)
    owner_hot = iota((n, count), 0) == owner
    lane_hot = iota((LANES, count), 0) == place

    loads[1].wait()
    key = ((cid_ref[...] // n) * big + rank_ref[...] + 1).astype(jnp.float32)
    keys = dot(jnp.where(owner_hot, key, 0.0), lane_hot.astype(jnp.float32), NT, EXACT)
    lanes = iota((n, LANES), 1)
    missed = jnp.max(jnp.where(place >= sum(chunks), 1.0, 0.0), axis=1, keepdims=True)
    keys = jnp.where(lanes < sum(chunks), keys, jnp.where(lanes == LANES - 1, missed, 0.0))
    keys_out[...] = keys.reshape(n, 1, LANES)

    loads[2].wait()
    values = emb_ref[...].astype(jnp.float32)
    unit = (
        values * lax.rsqrt(jnp.sum(values * values, axis=1, keepdims=True) + epsilon)
    ).astype(jnp.bfloat16)

    def pack(piece, turn):
        size = chunks[piece]
        base = quarter_of(turn) * quarter
        local = place - starts[piece]
        slot = jnp.where((local >= 0) & (local < size), (owner - base) * size + local, -1)
        hot = (iota((quarter * size, count), 0) == slot).astype(jnp.bfloat16)
        packed = dot(hot, unit, NN).astype(jnp.bfloat16)
        rows_out[piece][pl.ds(base, quarter)] = packed.reshape(quarter, size, width)

    def send_keys(peer):
        return remote(
            keys_out.at[peer], keys_in.at[me], keys_out_sem.at[peer], keys_in_sem.at[me], peer
        )

    def take_keys(peer):
        return remote(
            keys_out.at[peer], keys_in.at[peer], keys_out_sem.at[peer], keys_in_sem.at[peer], peer
        )

    def send_rows(piece, peer):
        return remote(
            rows_out[piece].at[peer], rows_in[piece].at[me],
            rows_out_sem.at[piece, peer], rows_in_sem.at[piece, me], peer,
        )

    def take_rows(piece, peer):
        return remote(
            rows_out[piece].at[peer], rows_in[piece].at[peer],
            rows_out_sem.at[piece, peer], rows_in_sem.at[piece, peer], peer,
        )

    def send_best(peer):
        return remote(
            best_out.at[peer], best_in.at[me], best_out_sem.at[peer], best_in_sem.at[me], peer
        )

    def take_best(peer):
        return remote(
            best_out.at[peer], best_in.at[peer], best_out_sem.at[peer], best_in_sem.at[peer], peer
        )

    own = [
        pltpu.make_async_copy(rows_out[piece].at[me], rows_in[piece].at[me], own_sem.at[piece])
        for piece in range(pieces)
    ]
    own_keys = pltpu.make_async_copy(keys_out.at[me], keys_in.at[me], own_sem.at[pieces])
    own_best = pltpu.make_async_copy(best_out.at[me], best_in.at[me], own_sem.at[pieces + 1])

    for turn in range(4):
        pack(0, turn)
    pl.semaphore_wait(barrier, n - 1)
    for piece in range(pieces):
        for turn in range(4):
            if piece > 0:
                pack(piece, turn)
            each(lambda peer: send_rows(piece, peer).start(), (turn,))
        own[piece].start()
        if piece == 0:
            each(lambda peer: send_keys(peer).start())
            own_keys.start()

    each(lambda peer: take_keys(peer).wait_recv())
    own_keys.wait()
    got = keys_in[...].reshape(n, LANES)
    over_ref[0, 0] = jnp.max(jnp.where(lanes == LANES - 1, got, 0.0))
    key_rows, key_columns, floors, spreads, sources = [], [], [], [], []
    for size, start in zip(chunks, starts):
        block = n * size
        source = (iota((n, block), 1) // size == iota((n, block), 0)).astype(jnp.float32)
        spread = iota((LANES, block), 0) == iota((LANES, block), 1) % size + start
        by_lane = dot(got, source, TN, EXACT)
        row = jnp.sum(jnp.where(spread, by_lane, 0.0), axis=0, keepdims=True)
        key_rows.append(row)
        key_columns.append(column(row))
        floors.append(jnp.floor(row * (1.0 / big)) * big)
        spreads.append(spread.astype(jnp.float32))
        sources.append(source)

    best = [jnp.full((1, n * size), -1.0, jnp.float32) for size in chunks]
    for piece, size in enumerate(chunks):
        each(lambda peer: take_rows(piece, peer).wait_recv())
        own[piece].wait()
        here = rows_in[piece][...].reshape(n * size, width)
        for other in range(piece + 1):
            there = rows_in[other][...].reshape(n * chunks[other], width)
            pairs = [(here, piece, there, other)]
            if other != piece:
                pairs.append((there, other, here, piece))
            for members, m, queries, q in pairs:
                scores = dot(members, queries, NT)
                allowed = (key_columns[m] > floors[q]) & (key_columns[m] < key_rows[q])
                top = jnp.max(jnp.where(allowed, scores, -1.0), axis=0, keepdims=True)
                best[q] = jnp.maximum(best[q], top)
    answer = jnp.zeros((n, LANES), jnp.float32)
    for piece in range(pieces):
        answer = answer + dot(sources[piece] * best[piece], spreads[piece], NT, EXACT)
    best_out[...] = answer.reshape(n, 1, LANES)
    each(lambda peer: send_best(peer).start(), (2, 0, 1, 3))
    own_best.start()

    each(lambda peer: take_keys(peer).wait_send())
    for piece in range(pieces):
        each(lambda peer: take_rows(piece, peer).wait_send())
    each(lambda peer: take_best(peer).wait_recv())
    own_best.wait()
    by_row = dot(best_in[...].reshape(n, LANES), owner_hot.astype(jnp.float32), TN, EXACT)
    out_ref[...] = jnp.sum(jnp.where(lane_hot, by_row, 0.0), axis=0, keepdims=True)
    each(lambda peer: take_best(peer).wait_send())


def exchange(embeddings, cluster_ids, ranks, chunks, number):
    splits = lax.axis_size("split")
    n = lax.axis_size("loader") * splits
    count, width = embeddings.shape
    big = 1 << (n * count + 1).bit_length()
    dma = pltpu.SemaphoreType.DMA
    vmem = pl.BlockSpec(memory_space=pltpu.VMEM)
    rows = [pltpu.VMEM((n, size, width), jnp.bfloat16) for size in chunks]
    return pl.pallas_call(
        functools.partial(kernel, n, splits, chunks, big),
        out_shape=(
            jax.ShapeDtypeStruct((1, count), jnp.float32),
            jax.ShapeDtypeStruct((1, 1), jnp.float32),
        ),
        in_specs=[pl.BlockSpec(memory_space=pl.ANY)] * 3,
        out_specs=(vmem, pl.BlockSpec(memory_space=pltpu.SMEM)),
        scratch_shapes=[
            *rows,
            *rows,
            *[pltpu.VMEM((n, 1, LANES), jnp.float32)] * 4,
            dma((len(chunks), n)),
            dma((len(chunks), n)),
            *[dma((n,))] * 4,
            dma((len(chunks) + 2,)),
            pltpu.VMEM((count, width), embeddings.dtype),
            pltpu.VMEM((1, count), jnp.int32),
            pltpu.VMEM((1, count), jnp.int32),
            dma((3,)),
        ],
        compiler_params=pltpu.CompilerParams(collective_id=number, has_side_effects=True, vmem_limit_bytes=None if number == 0 else 67_043_328),
    )(embeddings, cluster_ids, ranks)


def two_sizes(embeddings, cluster_ids, ranks):
    n = lax.axis_size("loader") * lax.axis_size("split")
    count = embeddings.shape[0]
    cluster_ids, ranks = cluster_ids.reshape(1, count), ranks.reshape(1, count)
    most = CLUSTERS // n * CAP
    small, over = exchange(embeddings, cluster_ids, ranks, (TILE, most * 3 // 4 - TILE), 0)
    out = lax.cond(
        over[0, 0] > 0.0,
        lambda: exchange(embeddings, cluster_ids, ranks, (TILE, most - TILE), 1)[0],
        lambda: small,
    )
    return out.reshape(count)


def tile_scores(queries, remote):
    return jnp.einsum("kqd,kmd->kqm", queries, remote, preferred_element_type=jnp.float32)


def row_maxima(scores, query_rank, member_rank):
    allowed = (member_rank[:, None, :] >= 0) & (member_rank[:, None, :] < query_rank[:, :, None])
    return jnp.max(jnp.where(allowed, scores, jnp.float32(-1.0)), axis=2)


def small_tiles(embeddings, cluster_ids, ranks):
    loader_count = lax.axis_size("loader")
    split_count = lax.axis_size("split")
    rows_here = embeddings.shape[0]
    width = embeddings.shape[1]
    values = embeddings.astype(jnp.float32)
    unit = (values * lax.rsqrt(jnp.sum(values * values, axis=1, keepdims=True) + epsilon)).astype(
        jnp.bfloat16
    )
    cluster = cluster_ids[:, 0]
    row_index = jnp.arange(rows_here, dtype=jnp.int32)
    same_cluster = cluster[:, None] == cluster[None, :]
    earlier = row_index[None, :] < row_index[:, None]
    position = jnp.sum((same_cluster & earlier).astype(jnp.int32), axis=1)
    slot_count = CLUSTERS * CAP
    device_count = loader_count * split_count
    owner_flat = cluster % device_count
    cluster_slot = cluster // device_count
    owned = CLUSTERS // device_count
    target = (
        (cluster_slot * loader_count + owner_flat // split_count) * split_count
        + owner_flat % split_count
    ) * CAP + position
    send_rows = (
        jnp.zeros((slot_count, width), jnp.bfloat16)
        .at[target]
        .set(unit)
        .reshape(owned, loader_count, split_count, CAP, width)
    )
    send_rank = (
        jnp.full((slot_count,), -1, jnp.int32)
        .at[target]
        .set(ranks)
        .reshape(owned, loader_count, split_count, CAP)
    )

    def swap(block):
        return lax.all_to_all(
            lax.all_to_all(block, "loader", split_axis=1, concat_axis=1, tiled=True),
            "split",
            split_axis=2,
            concat_axis=2,
            tiled=True,
        )

    members = swap(send_rows).reshape(owned, -1, width)
    member_rank = swap(send_rank).reshape(owned, -1)
    best = row_maxima(tile_scores(members, members), member_rank, member_rank)
    returned = swap(best.reshape(owned, loader_count, split_count, CAP))
    return returned.reshape(-1)[target]


def shards(embeddings, cluster_ids, ranks):
    n = lax.axis_size("loader") * lax.axis_size("split")
    fits = n % 4 == 0 and CLUSTERS // n * CAP == 2 * TILE
    return (two_sizes if fits else small_tiles)(embeddings, cluster_ids, ranks)


def solution(mesh):
    return jax.shard_map(
        shards,
        mesh=mesh,
        in_specs=(
            P(("loader", "split"), None),
            P(("loader", "split"), None),
            P(("loader", "split")),
        ),
        out_specs=P(("loader", "split")),
        check_vma=False,
    )
```

profile of v0, /device:TPU:0, one launch (start us, length us, event | category | flops | bytes accessed | tf_op | source)
XLA Modules:
  0.0 45.5 jit_solution(14698698181544603205)
XLA Ops:
  0.0 44.2 %shard_map.39 = (f32[1,512]{1,0:T(1,128)S(1)}, f32[1,1]{1,0:T(1,128)}) custom-call(bf16[512,768]{1,0:T(8,128)(2,1)} %emb_hbm.1, s32[1,512]{1,0:T(1,128)} %bitcast.2.cid_hbm, s32[1,512]{1,0:T(1,128)} %bitcast.3.rank_hbm), custom_call_target="tpu_custom_call" | custom-call | tf_op jit(solution)/shard_map/pallas_call | solution.py:228
  44.9 0.6 %copy.10 = f32[512]{0:T(512)} copy(f32[512]{0:T(512)S(1)} %get-tuple-element.25) | data formatting | bytes 4096
  (1 shorter events, 0.0 us)
where the time goes:
time: 45.6 us; the launch traced here: 45.5 us
  Pallas kernels  44.2 us (97%)
  between operations  0.64 us (1%)
  local copies, waits for them, and re-layouts  0.58 us (1%)
    pallas_call x1, Pallas kernels, exchange(): pl.pallas_call(functools.partial(kernel, n, splits, chunks, big), out_sha...  44.2 us

commit v1 on v0

--- a/solution.py
+++ b/solution.py
@@ -118,34 +118,37 @@
 
     def send_keys(peer):
         return remote(
-            keys_out.at[peer], keys_in.at[me], keys_out_sem.at[peer], keys_in_sem.at[me], peer
-        )
-
-    def take_keys(peer):
-        return remote(
-            keys_out.at[peer], keys_in.at[peer], keys_out_sem.at[peer], keys_in_sem.at[peer], peer
+            keys_out.at[peer], keys_in.at[me], keys_out_sem, keys_in_sem, peer
+        )
+
+    others = pl.ds(0, n - 1)
+    next_one = (me + 1) % n
+
+    def take_keys():
+        return remote(
+            keys_out.at[others], keys_in.at[others], keys_out_sem, keys_in_sem, next_one
         )
 
     def send_rows(piece, peer):
         return remote(
             rows_out[piece].at[peer], rows_in[piece].at[me],
-            rows_out_sem.at[piece, peer], rows_in_sem.at[piece, me], peer,
-        )
-
-    def take_rows(piece, peer):
-        return remote(
-            rows_out[piece].at[peer], rows_in[piece].at[peer],
-            rows_out_sem.at[piece, peer], rows_in_sem.at[piece, peer], peer,
+            rows_out_sem.at[piece], rows_in_sem.at[piece], peer,
+        )
+
+    def take_rows(piece):
+        return remote(
+            rows_out[piece].at[others], rows_in[piece].at[others],
+            rows_out_sem.at[piece], rows_in_sem.at[piece], next_one,
         )
 
     def send_best(peer):
         return remote(
-            best_out.at[peer], best_in.at[me], best_out_sem.at[peer], best_in_sem.at[me], peer
-        )
-
-    def take_best(peer):
-        return remote(
-            best_out.at[peer], best_in.at[peer], best_out_sem.at[peer], best_in_sem.at[peer], peer
+            best_out.at[peer], best_in.at[me], best_out_sem, best_in_sem, peer
+        )
+
+    def take_best():
+        return remote(
+            best_out.at[others], best_in.at[others], best_out_sem, best_in_sem, next_one
         )
 
     own = [
@@ -168,7 +171,7 @@
             each(lambda peer: send_keys(peer).start())
             own_keys.start()
 
-    each(lambda peer: take_keys(peer).wait_recv())
+    take_keys().wait_recv()
     own_keys.wait()
     got = keys_in[...].reshape(n, LANES)
     over_ref[0, 0] = jnp.max(jnp.where(lanes == LANES - 1, got, 0.0))
@@ -187,7 +190,7 @@
 
     best = [jnp.full((1, n * size), -1.0, jnp.float32) for size in chunks]
     for piece, size in enumerate(chunks):
-        each(lambda peer: take_rows(piece, peer).wait_recv())
+        take_rows(piece).wait_recv()
         own[piece].wait()
         here = rows_in[piece][...].reshape(n * size, width)
         for other in range(piece + 1):
@@ -207,14 +210,14 @@
     each(lambda peer: send_best(peer).start(), (2, 0, 1, 3))
     own_best.start()
 
-    each(lambda peer: take_keys(peer).wait_send())
+    take_keys().wait_send()
     for piece in range(pieces):
-        each(lambda peer: take_rows(piece, peer).wait_send())
-    each(lambda peer: take_best(peer).wait_recv())
+        take_rows(piece).wait_send()
+    take_best().wait_recv()
     own_best.wait()
     by_row = dot(best_in[...].reshape(n, LANES), owner_hot.astype(jnp.float32), TN, EXACT)
     out_ref[...] = jnp.sum(jnp.where(lane_hot, by_row, 0.0), axis=0, keepdims=True)
-    each(lambda peer: take_best(peer).wait_send())
+    take_best().wait_send()
 
 
 def exchange(embeddings, cluster_ids, ranks, chunks, number):
@@ -237,9 +240,9 @@
             *rows,
             *rows,
             *[pltpu.VMEM((n, 1, LANES), jnp.float32)] * 4,
-            dma((len(chunks), n)),
-            dma((len(chunks), n)),
-            *[dma((n,))] * 4,
+            dma((len(chunks),)),
+            dma((len(chunks),)),
+            *[dma] * 4,
             dma((len(chunks) + 2,)),
             pltpu.VMEM((count, width), embeddings.dtype),
             pltpu.VMEM((1, count), jnp.int32),

time: 45.6 us -> 42.7 us (0.936)
  Pallas kernels: 44.2 us -> 41.3 us
    pallas_call x1, Pallas kernels: 44.2 us -> 41.3 us  [exchange(): pl.pallas_call(functools.partial(kernel, n, splits, chunks, big), out_sha...]
where the time goes in v1:
time: 42.7 us; the launch traced here: 42.6 us
  Pallas kernels  41.3 us (97%)
  between operations  0.64 us (1%)
  local copies, waits for them, and re-layouts  0.58 us (1%)
    pallas_call x1, Pallas kernels, exchange(): pl.pallas_call(functools.partial(kernel, n, splits, chunks, big), out_sha...  41.3 us

profile of v1, /device:TPU:0, one launch (start us, length us, event | category | flops | bytes accessed | tf_op | source)
XLA Modules:
  0.0 42.6 jit_solution(701626025376745834)
XLA Ops:
  0.0 41.3 %shard_map.39 = (f32[1,512]{1,0:T(1,128)S(1)}, f32[1,1]{1,0:T(1,128)}) custom-call(bf16[512,768]{1,0:T(8,128)(2,1)} %emb_hbm.1, s32[1,512]{1,0:T(1,128)} %bitcast.2.cid_hbm, s32[1,512]{1,0:T(1,128)} %bitcast.3.rank_hbm), custom_call_target="tpu_custom_call" | custom-call | tf_op jit(solution)/shard_map/pallas_call | solution.py:231
  42.0 0.6 %copy.10 = f32[512]{0:T(512)} copy(f32[512]{0:T(512)S(1)} %get-tuple-element.25) | data formatting | bytes 4096
  (1 shorter events, 0.0 us)
